TPU v7x, 32 devices: a whole 2x2x4 slice. The times are simulated.
32 devices in a mesh: rep: 4 (over x, core), fsdp: 8 (over z, y).
Axes of the slice: x: 2, y: 2, z: 4, core: 2. Of those that a mesh axis runs over, the one named last changes fastest.
Arguments:
- features: bfloat16 [4096, 1280], P(('rep', 'fsdp')), may hold values from -6 to 6
- cotangent: bfloat16 [4096, 1280], P(('rep', 'fsdp')), may hold values from -1 to 1
- clip_lengths: int32 [4, 8], P('rep'), may hold values from 96 to 128, as said below
- group_clips: int32 [4], P('rep'), may hold values from 6 to 8, as said below
- outer_attention: float32 [2, 1280, 5120], P(None, 'fsdp')
- outer_feedforward: float32 [2, 1280, 10240], P(None, 'fsdp')
- outer_vectors: float32 [2, 12, 1280], P(None, None, 'fsdp')
- moments_attention: float32 [4, 2, 1280, 5120], P('rep', None, 'fsdp')
- moments_feedforward: float32 [4, 2, 1280, 10240], P('rep', None, 'fsdp')
- moments_vectors: float32 [4, 2, 12, 1280], P('rep', None, None, 'fsdp')
Outputs:
- block_output: bfloat16 [4096, 1280], P(('rep', 'fsdp'))
- input_grad: float32 [4096, 1280], P(('rep', 'fsdp'))
- group_attention: float32 [4, 3, 1280, 5120], P('rep', None, 'fsdp')
- group_feedforward: float32 [4, 3, 1280, 10240], P('rep', None, 'fsdp')
- group_vectors: float32 [4, 3, 12, 1280], P('rep', None, None, 'fsdp')
- group_weights: float32 [4, 1280, 15372], P('rep', 'fsdp')
- next_attention: float32 [3, 1280, 5120], P(None, 'fsdp')
- next_feedforward: float32 [3, 1280, 10240], P(None, 'fsdp')
- next_vectors: float32 [3, 12, 1280], P(None, None, 'fsdp')
- copy_attention: bfloat16 [1280, 5120], P('fsdp')
- copy_feedforward: bfloat16 [1280, 10240], P('fsdp')
- copy_vectors: bfloat16 [12, 1280], P(None, 'fsdp')
Inputs may be any that keep to these rules, and one draw needn't show every extreme that they name: `clip_lengths`: some clip has exactly 128 valid tokens and some exactly 96. Group g holds clips in its slots 0 to group_clips[g] - 1 and none in the others; some group has all 8 and some 8 - 2.
All inputs are finite; a program needn't handle non-finite values.
Results may differ from a plain program's by a relative error of at most 0.012.
The roundings to bfloat16 on the way count: a program that leaves them out, or rounds other values in their place, can miss the bound.
Values may be sent and summed in bfloat16 or wider, within the bound.
A program may use at most 448 MiB of HBM per device.

v0:
```python
from functools import partial
import jax
import jax.numpy as jnp
from jax import lax
from jax.sharding import PartitionSpec as P

D = 1280
HEADS = 16
HD = 80
FF = 5120
STEP = 3
NORM_EPS = 1e-05
MASKED = -1e30
ADAM_RATE = 0.03
ADAM_DECAY = 0.1
ADAM_BETA = 0.5
ADAM_EPS = 1e-08
OUTER_RATE = 0.7
OUTER_MOMENTUM = 0.5


def contract_last(left, right):
    return lax.dot_general(
        left, right, (((1,), (1,)), ((), ())), preferred_element_type=jnp.float32
    )


def contract_rows(left, right):
    return lax.dot_general(
        left, right, (((0,), (0,)), ((), ())), preferred_element_type=jnp.float32
    )


def normalize(inputs, gain_row, shift_row):
    average = jnp.mean(inputs, axis=-1, keepdims=True)
    centered = inputs - average
    reciprocal = lax.rsqrt(jnp.mean(centered * centered, axis=-1, keepdims=True) + NORM_EPS)
    unit_rows = centered * reciprocal
    return (unit_rows * gain_row + shift_row, unit_rows, reciprocal)


def normalize_back(incoming, unit_rows, reciprocal, gain_row):
    scaled = incoming * gain_row
    centered = scaled - jnp.mean(scaled, axis=-1, keepdims=True)
    return reciprocal * (
        centered - unit_rows * jnp.mean(scaled * unit_rows, axis=-1, keepdims=True)
    )


def adamw_step(weight, gradient, moments, decay_rate):
    first_moment = ADAM_BETA * moments[0] + (1.0 - ADAM_BETA) * gradient
    second_moment = ADAM_BETA * moments[1] + (1.0 - ADAM_BETA) * gradient * gradient
    correction = 1.0 - ADAM_BETA**STEP
    direction = first_moment / correction / (jnp.sqrt(second_moment / correction) + ADAM_EPS)
    return (weight - ADAM_RATE * (direction + decay_rate * weight), first_moment, second_moment)


def outer_step(master, mean_delta, momentum_old):
    momentum = OUTER_MOMENTUM * momentum_old - mean_delta
    outer_next = master - OUTER_RATE * (OUTER_MOMENTUM * momentum - mean_delta)
    return jnp.stack([mean_delta, momentum, outer_next])


def shards(
    features,
    cotangent,
    clip_lengths,
    group_clips,
    outer_attention,
    outer_feedforward,
    outer_vectors,
    moments_attention,
    moments_feedforward,
    moments_vectors,
):
    tokens_here = features.shape[0]
    scale = HD ** (-0.5)
    clip_slot = lax.axis_index("fsdp")
    clip_length = lax.dynamic_index_in_dim(clip_lengths[0], clip_slot, keepdims=False)
    live_clip = clip_slot < group_clips[0]
    positions = jnp.arange(tokens_here, dtype=jnp.int32)
    key_valid = positions < clip_length
    row_valid = key_valid & live_clip
    masters = (outer_attention[0], outer_feedforward[0], outer_vectors[0])
    copies = (
        masters[0].astype(jnp.bfloat16),
        masters[1].astype(jnp.bfloat16),
        masters[2].astype(jnp.bfloat16),
    )
    full_attention, full_feedforward, full_vectors = (
        lax.all_gather(copies[0], "fsdp", axis=0, tiled=True),
        lax.all_gather(copies[1], "fsdp", axis=0, tiled=True),
        lax.all_gather(copies[2], "fsdp", axis=1, tiled=True),
    )
    vectors = full_vectors.astype(jnp.float32)
    inputs = features.astype(jnp.float32)
    normed_one, unit_one, scale_one = normalize(inputs, vectors[0], vectors[1])
    layer_one = normed_one.astype(jnp.bfloat16)
    qkv_bias = jnp.concatenate([vectors[2], jnp.zeros_like(vectors[2]), vectors[3]])
    projected = (
        jnp.dot(layer_one, full_attention[:, : 3 * D], preferred_element_type=jnp.float32)
        + qkv_bias
    ).astype(jnp.bfloat16)
    query_heads = projected[:, :D].reshape(tokens_here, HEADS, HD)
    key_heads = projected[:, D : 2 * D].reshape(tokens_here, HEADS, HD)
    value_heads = projected[:, 2 * D :].reshape(tokens_here, HEADS, HD)

    def score_block():
        raw_scores = (
            jnp.einsum("qhd,khd->hqk", query_heads, key_heads, preferred_element_type=jnp.float32)
            * scale
        )
        return jnp.where(key_valid[None, None, :], raw_scores, MASKED)

    scores = score_block()
    top_score = jnp.max(scores, axis=-1, keepdims=True)
    exponent = jnp.exp(scores - top_score)
    totals = jnp.sum(exponent, axis=-1, keepdims=True)
    attention_probs = exponent / totals
    log_totals = top_score + jnp.log(totals)
    attended = jnp.einsum(
        "hqk,khd->qhd",
        attention_probs.astype(jnp.bfloat16),
        value_heads,
        preferred_element_type=jnp.float32,
    )
    attended = attended.reshape(tokens_here, D).astype(jnp.bfloat16)
    attention_branch = contract_last(attended, full_attention[:, 3 * D :]) + vectors[4]
    middle = inputs + attention_branch
    normed_two, unit_two, scale_two = normalize(middle, vectors[5], vectors[6])
    layer_two = normed_two.astype(jnp.bfloat16)
    pre_activation = jnp.dot(
        layer_two, full_feedforward[:, :FF], preferred_element_type=jnp.float32
    ) + vectors[8:].reshape(FF)
    activation, gelu_backward = jax.vjp(partial(jax.nn.gelu, approximate=False), pre_activation)
    activation_low = activation.astype(jnp.bfloat16)
    feedforward_branch = contract_last(activation_low, full_feedforward[:, FF:]) + vectors[7]
    block_output = (middle + feedforward_branch).astype(jnp.bfloat16)
    back_attention, back_feedforward, back_vectors = (
        lax.all_gather(copies[0], "fsdp", axis=0, tiled=True),
        lax.all_gather(copies[1], "fsdp", axis=0, tiled=True),
        lax.all_gather(copies[2], "fsdp", axis=1, tiled=True),
    )
    gain_rows = back_vectors.astype(jnp.float32)
    upstream = cotangent.astype(jnp.float32) * row_valid[:, None].astype(jnp.float32)
    upstream_low = upstream.astype(jnp.bfloat16)
    grad_down_bias = jnp.sum(upstream_low, axis=0, dtype=jnp.float32)
    grad_activation = jnp.dot(
        upstream_low, back_feedforward[:, FF:], preferred_element_type=jnp.float32
    )
    grad_pre = gelu_backward(grad_activation)[0].astype(jnp.bfloat16)
    grad_up_bias = jnp.sum(grad_pre, axis=0, dtype=jnp.float32)
    grad_two = contract_last(grad_pre, back_feedforward[:, :FF])
    grad_gain_two = jnp.sum(grad_two * unit_two, axis=0)
    grad_shift_two = jnp.sum(grad_two, axis=0)
    grad_middle = upstream + normalize_back(grad_two, unit_two, scale_two, gain_rows[5])
    middle_low = grad_middle.astype(jnp.bfloat16)
    grad_out_bias = jnp.sum(middle_low, axis=0, dtype=jnp.float32)
    grad_attended = jnp.dot(
        middle_low, back_attention[:, 3 * D :], preferred_element_type=jnp.float32
    ).astype(jnp.bfloat16)
    grad_heads = grad_attended.reshape(tokens_here, HEADS, HD)
    attention_probs = jnp.exp(score_block() - log_totals)
    grad_probs = jnp.einsum(
        "qhd,khd->hqk", grad_heads, value_heads, preferred_element_type=jnp.float32
    )
    row_dot = jnp.sum(attention_probs * grad_probs, axis=-1, keepdims=True)
    grad_scores = (attention_probs * (grad_probs - row_dot)).astype(jnp.bfloat16)
    grad_queries = (
        jnp.einsum("hqk,khd->qhd", grad_scores, key_heads, preferred_element_type=jnp.float32)
        * scale
    ).reshape(tokens_here, D)
    grad_keys = (
        jnp.einsum("hqk,qhd->khd", grad_scores, query_heads, preferred_element_type=jnp.float32)
        * scale
    ).reshape(tokens_here, D)
    grad_values = jnp.einsum(
        "hqk,qhd->khd",
        attention_probs.astype(jnp.bfloat16),
        grad_heads,
        preferred_element_type=jnp.float32,
    ).reshape(tokens_here, D)
    grad_qkv = jnp.concatenate([grad_queries, grad_keys, grad_values], axis=1).astype(jnp.bfloat16)
    grad_query_bias = jnp.sum(grad_qkv[:, :D], axis=0, dtype=jnp.float32)
    grad_value_bias = jnp.sum(grad_qkv[:, 2 * D :], axis=0, dtype=jnp.float32)
    grad_one = contract_last(grad_qkv, back_attention[:, : 3 * D])
    grad_gain_one = jnp.sum(grad_one * unit_one, axis=0)
    grad_shift_one = jnp.sum(grad_one, axis=0)
    input_grad = grad_middle + normalize_back(grad_one, unit_one, scale_one, gain_rows[0])
    vector_rows = jnp.stack(
        [
            grad_gain_one,
            grad_shift_one,
            grad_query_bias,
            grad_value_bias,
            grad_out_bias,
            grad_gain_two,
            grad_shift_two,
            grad_down_bias,
        ]
    )
    grad_vectors = jnp.concatenate([vector_rows, grad_up_bias.reshape(4, D)], axis=0)
    owned_attention = lax.psum_scatter(
        jnp.concatenate(
            [contract_rows(layer_one, grad_qkv), contract_rows(middle_low, attended)], axis=1
        ),
        "fsdp",
        scatter_dimension=0,
        tiled=True,
    )
    owned_feedforward = lax.psum_scatter(
        jnp.concatenate(
            [contract_rows(layer_two, grad_pre), contract_rows(upstream_low, activation_low)],
            axis=1,
        ),
        "fsdp",
        scatter_dimension=0,
        tiled=True,
    )
    owned_vectors = lax.psum_scatter(grad_vectors, "fsdp", scatter_dimension=1, tiled=True)
    new_attention, first_attention, second_attention = adamw_step(
        masters[0], owned_attention, moments_attention[0], ADAM_DECAY
    )
    new_feedforward, first_feedforward, second_feedforward = adamw_step(
        masters[1], owned_feedforward, moments_feedforward[0], ADAM_DECAY
    )
    new_vectors, first_vectors, second_vectors = adamw_step(
        masters[2], owned_vectors, moments_vectors[0], 0.0
    )
    summed = (
        lax.psum_scatter(
            (new_attention - masters[0]).astype(jnp.bfloat16),
            "rep",
            scatter_dimension=1,
            tiled=True,
        ).astype(jnp.float32),
        lax.psum_scatter(
            (new_feedforward - masters[1]).astype(jnp.bfloat16),
            "rep",
            scatter_dimension=1,
            tiled=True,
        ).astype(jnp.float32),
        lax.psum_scatter(
            (new_vectors - masters[2]).astype(jnp.bfloat16), "rep", scatter_dimension=0, tiled=True
        ).astype(jnp.float32),
    )
    replicas = lax.axis_size("rep")
    replica_index = lax.axis_index("rep")
    attention_cols = 4 * D // replicas
    feedforward_cols = 2 * FF // replicas
    vector_count = 12 // replicas

    def owned_part(array, dim, count):
        return lax.dynamic_slice_in_dim(array, replica_index * count, count, dim)

    part_attention = outer_step(
        owned_part(masters[0], 1, attention_cols),
        summed[0] / replicas,
        owned_part(outer_attention[1], 1, attention_cols),
    )
    part_feedforward = outer_step(
        owned_part(masters[1], 1, feedforward_cols),
        summed[1] / replicas,
        owned_part(outer_feedforward[1], 1, feedforward_cols),
    )
    part_vectors = outer_step(
        owned_part(masters[2], 0, vector_count),
        summed[2] / replicas,
        owned_part(outer_vectors[1], 0, vector_count),
    )
    next_attention, next_feedforward, next_vectors = (
        lax.all_gather(part_attention, "rep", axis=2, tiled=True),
        lax.all_gather(part_feedforward, "rep", axis=2, tiled=True),
        lax.all_gather(part_vectors, "rep", axis=1, tiled=True),
    )
    copy_attention = next_attention[2].astype(jnp.bfloat16)
    copy_feedforward = next_feedforward[2].astype(jnp.bfloat16)
    copy_vectors = next_vectors[2].astype(jnp.bfloat16)
    group_attention = jnp.stack([owned_attention, first_attention, second_attention])[None]
    group_feedforward = jnp.stack([owned_feedforward, first_feedforward, second_feedforward])[None]
    group_vectors = jnp.stack([owned_vectors, first_vectors, second_vectors])[None]
    group_weights = jnp.concatenate([new_attention, new_feedforward, new_vectors.T], axis=1)[None]
    return (
        block_output,
        input_grad,
        group_attention,
        group_feedforward,
        group_vectors,
        group_weights,
        next_attention,
        next_feedforward,
        next_vectors,
        copy_attention,
        copy_feedforward,
        copy_vectors,
    )


def solution(mesh):
    in_specs = (
        P(("rep", "fsdp"), None),
        P(("rep", "fsdp"), None),
        P("rep", None),
        P("rep"),
        P(None, "fsdp", None),
        P(None, "fsdp", None),
        P(None, None, "fsdp"),
        P("rep", None, "fsdp", None),
        P("rep", None, "fsdp", None),
        P("rep", None, None, "fsdp"),
    )
    out_specs = (
        P(("rep", "fsdp"), None),
        P(("rep", "fsdp"), None),
        P("rep", None, "fsdp", None),
        P("rep", None, "fsdp", None),
        P("rep", None, None, "fsdp"),
        P("rep", "fsdp", None),
        P(None, "fsdp", None),
        P(None, "fsdp", None),
        P(None, None, "fsdp"),
        P("fsdp", None),
        P("fsdp", None),
        P(None, "fsdp"),
    )
    return jax.shard_map(shards, mesh=mesh, in_specs=in_specs, out_specs=out_specs, check_vma=False)
```

profile of v0, /device:TPU:0, one launch (start us, length us, event | category | flops | bytes accessed | tf_op | source)
XLA Modules:
  0.0 2351.6 jit_solution(7769149582330624274)
XLA Ops:
  10.6 5.0 bitcast_convert_fusion
  17.1 33.6 %all-gather = bf16[8,160,12]{1,2,0:T(8,128)(2,1)S(1)} all-gather(bf16[1,160,12]{1,2,0:T(8,128)(2,1)S(1)} %copy.142), channel_id=1, replica_groups=mesh['rep'=4,'fsdp'=8] {'fsdp'}, dimensions={0}, use_global_device_ids=true | all-gather | bytes 34560 | tf_op jit(solution)/shard_map/all_gather | solution.py:93
  54.6 141.9 %all-gather.6.cloned.1.call-done = bf16[1280,5120]{1,0:T(8,128)(2,1)} async-done(((bf16[160,5120]{1,0:T(8,128)(2,1)}), bf16[1280,5120]{1,0:T(8,128)(2,1)}) %all-gather.6.cloned.1.call-update) | async-done | bytes 13107216 | tf_op jit(solution)/shard_map/all_gather | solution.py:91
  196.5 5.3 fusion.22
  207.5 489.4 %all-gather.8.cloned.1.call-done = bf16[1280,10240]{1,0:T(8,128)(2,1)} async-done(((bf16[160,10240]{1,0:T(8,128)(2,1)}), bf16[1280,10240]{1,0:T(8,128)(2,1)}) %all-gather.8.cloned.1.call-update) | async-done | bytes 26214416 | tf_op jit(solution)/shard_map/all_gather | solution.py:92
  696.8 5.9 fusion.16
  702.8 11.3 convert_reduce_fusion
  714.1 8.4 multiply_reduce_fusion.1
  736.2 9.2 pad_maximum_fusion.1
  745.6 13.1 fusion.115
  758.6 12.3 fusion.110
  770.9 34.1 %pad_maximum_fusion = f32[1280,10240]{1,0:T(8,128)} fusion(f32[1280,5120]{1,0:T(8,128)} %fusion.110, f32[1280,5120]{1,0:T(8,128)} %fusion.115), kind=kLoop, calls=%fused_computation | loop fusion | flops 13107200 | bytes 104857600 | tf_op jit(solution)/shard_map/concatenate | solution.py:212
  805.1 358.9 %reduce-scatter.7.cloned.1.call-done = f32[160,5120]{1,0:T(8,128)} async-done(((f32[1280,5120]{1,0:T(8,128)}), f32[160,5120]{1,0:T(8,128)}) %reduce-scatter.7.cloned.1.call-update) | async-done | bytes 3276816 | tf_op jit(solution)/shard_map/reduce_scatter | solution.py:203
  1164.0 9.6 fusion.29
  1173.7 811.0 %reduce-scatter.9.cloned.1.call-done = f32[160,10240]{1,0:T(8,128)} async-done(((f32[1280,10240]{1,0:T(8,128)}), f32[160,10240]{1,0:T(8,128)}) %reduce-scatter.9.cloned.1.call-update) | async-done | bytes 6553616 | tf_op jit(solution)/shard_map/reduce_scatter | solution.py:211
  1984.6 18.2 fusion.15
  2003.2 6.5 fusion.117
  2009.7 6.0 fusion.87
  2021.1 12.6 fusion.116
  2033.6 22.6 reduce-scatter.15.cloned.1.call-done
  2066.4 13.2 fusion.54
  2079.6 42.7 %reduce-scatter.11.cloned.1.call-done = f32[12,160]{0,1:T(8,128)} async-done(((f32[12,1280]{0,1:T(8,128)}), f32[12,160]{0,1:T(8,128)}) %reduce-scatter.11.cloned.1.call-update) | async-done | bytes 7696 | tf_op jit(solution)/shard_map/reduce_scatter | solution.py:220
  2127.6 12.0 all-reduce
  2139.9 5.8 all_gather.26
  2146.3 8.3 maximum_bitcast_fusion.2
  2154.6 35.4 %all-gather.10.cloned.1.call-done = f32[3,160,5120]{2,1,0:T(8,128)} async-done(((f32[3,160,1280]{2,1,0:T(8,128)}), f32[3,160,5120]{2,1,0:T(8,128)}) %all-gather.10.cloned.1.call-update) | async-done | bytes 9830416 | tf_op jit(solution)/shard_map/all_gather | solution.py:272
  2193.4 19.0 maximum_bitcast_fusion
  2213.1 5.5 maximum_bitcast_fusion.1
  2218.6 97.3 %all-gather.12.cloned.1.call-done = f32[3,160,10240]{2,1,0:T(8,128)} async-done(((f32[3,160,2560]{2,1,0:T(8,128)}), f32[3,160,10240]{2,1,0:T(8,128)}) %all-gather.12.cloned.1.call-update) | async-done | bytes 19660816 | tf_op jit(solution)/shard_map/all_gather | solution.py:273
  2315.8 5.0 fusion.26
  2320.8 8.8 copy.180
  2329.6 15.0 copy.181
  (150 shorter events, 52.5 us)
Async XLA Ops:
  7.2 44.4 %copy-start = (s32[1,8]{1,0:T(1,128)S(1)}, s32[1,8]{1,0:T(1,128)}, u32[]{:S(2)}) copy-start(s32[1,8]{1,0:T(1,128)} %param.12) | copy-start | bytes 100
  7.2 189.3 %all-gather.6.cloned.1.call-start = ((), (), s32[]{:S(2)}) async-start(), calls=%async_computation.5 | async-start | bytes 14745600 | tf_op jit(solution)/shard_map/all_gather | solution.py:91
  10.6 686.3 %all-gather.8.cloned.1.call-start = ((), (), s32[]{:S(2)}) async-start(), calls=%async_computation.6 | async-start | bytes 29491200 | tf_op jit(solution)/shard_map/all_gather | solution.py:92
  15.6 38.6 %copy-start.5 = (bf16[128,1280]{1,0:T(8,128)(2,1)S(1)}, bf16[128,1280]{1,0:T(8,128)(2,1)}, u32[]{:S(2)}) copy-start(bf16[128,1280]{1,0:T(8,128)(2,1)} %param.10) | copy-start | bytes 983044
  15.6 1148.4 %reduce-scatter.7.cloned.1.call-start = ((), (), s32[]{:S(2)}) async-start(), calls=%async_computation.7 | async-start | bytes 29491200 | tf_op jit(solution)/shard_map/reduce_scatter | solution.py:203
  17.1 184.8 %copy-start.9 = (f32[1,12,160]{1,2,0:T(8,128)}, f32[1,12,160]{1,2,0:T(8,128)S(1)}, u32[]{:S(2)}) copy-start(f32[1,12,160]{1,2,0:T(8,128)S(1)} %copy.171) | copy-start | bytes 23044
  202.1 1.3 copy-start.11
  203.5 3.7 copy-start.12
  207.2 538.3 %copy-start.4 = (f32[128,1280]{1,0:T(8,128)}, f32[128,1280]{1,0:T(8,128)S(1)}, u32[]{:S(2)}) copy-start(f32[128,1280]{1,0:T(8,128)S(1)} %get-tuple-element.138) | copy-start | bytes 1966084
  696.8 5.9 copy-start.14
  702.8 11.3 copy-start.21
  714.1 8.4 copy-start.8
  729.6 3.7 copy-start.6
  731.2 1.1 copy-start.13
  745.5 13.2 copy-start.15
  745.5 1239.1 %reduce-scatter.9.cloned.1.call-start = ((), (), s32[]{:S(2)}) async-start(), calls=%async_computation.8 | async-start | bytes 58982400 | tf_op jit(solution)/shard_map/reduce_scatter | solution.py:211
  745.5 13.1 copy-start.22
  805.0 1212.5 %reduce-scatter.13.cloned.1.call-start = ((), (), s32[]{:S(2)}) async-start(), calls=%async_computation.10 | async-start | bytes 2048000 | tf_op jit(solution)/shard_map/reduce_scatter | solution.py:231
  1173.6 882.6 %reduce-scatter.15.cloned.1.call-start = ((), (), s32[]{:S(2)}) async-start(), calls=%async_computation.12 | async-start | bytes 4096000 | tf_op jit(solution)/shard_map/reduce_scatter | solution.py:237
  2002.9 119.4 %reduce-scatter.11.cloned.1.call-start = ((), (), s32[]{:S(2)}) async-start(), calls=%async_computation.9 | async-start | bytes 737280 | tf_op jit(solution)/shard_map/reduce_scatter | solution.py:220
  2003.2 6.5 copy-start.7
  2017.5 172.6 %all-gather.10.cloned.1.call-start = ((), (), s32[]{:S(2)}) async-start(), calls=%async_computation.11 | async-start | bytes 12288000 | tf_op jit(solution)/shard_map/all_gather | solution.py:272
  2021.0 294.8 %all-gather.12.cloned.1.call-start = ((), (), s32[]{:S(2)}) async-start(), calls=%async_computation.13 | async-start | bytes 24576000 | tf_op jit(solution)/shard_map/all_gather | solution.py:273
  2061.6 2.4 copy-start.20
  2061.6 4.8 copy-start.19
  2066.4 55.9 %copy-start.10 = (f32[1,12,160]{1,2,0:T(8,128)S(1)}, f32[1,12,160]{1,2,0:T(8,128)}, u32[]{:S(2)}) copy-start(f32[1,12,160]{1,2,0:T(8,128)} %copy-done.9) | copy-start | bytes 23044
  2066.4 79.9 %copy-start.2 = (f32[160,5120]{1,0:T(8,128)S(1)}, f32[160,5120]{1,0:T(8,128)}, u32[]{:S(2)}) copy-start(f32[160,5120]{1,0:T(8,128)} %reduce-scatter.7.cloned.1.call-done) | copy-start | bytes 9830404
  2145.7 9.0 copy-start.16
  2193.3 19.0 slice-start
  2193.3 19.0 slice-start.1
  2193.3 19.7 copy-start.3
  2329.6 15.0 copy-start.1
  (2 other events, 1.5 us)
Sparse Core Ops, SparseCore 0:
  10.8 185.6 all-gather.5
  198.6 498.2 all-gather.7
  745.6 418.3 reduce-scatter.6
  1167.8 816.8 reduce-scatter.8
  1987.6 27.6 reduce-scatter.12
  2017.7 38.5 reduce-scatter.14
  2059.5 62.7 reduce-scatter.10
  2123.9 66.1 all-gather.9
  2191.6 124.1 all-gather.11
where the time goes:
time: 2360 us; the launch traced here: 2350 us
  waiting for transfers between devices  2000 us (85%)
  other arithmetic  119 us (5%)
  matrix products  91.1 us (4%)
  local copies, waits for them, and re-layouts  74.3 us (3%)
  blocking collectives  51.4 us (2%)
    reduce_scatter x1, waiting for transfers between devices, shards(): lax.psum_scatter(jnp.concatenate([contract_rows(layer_two, grad_pre), con...  811 us
    all_gather x1, waiting for transfers between devices, shards(): lax.all_gather(copies[1], 'fsdp', axis=0, tiled=True)  489 us
    reduce_scatter x1, waiting for transfers between devices, shards(): lax.psum_scatter(jnp.concatenate([contract_rows(layer_one, grad_qkv), con...  359 us
    all_gather x1, waiting for transfers between devices, shards(): lax.all_gather(copies[0], 'fsdp', axis=0, tiled=True)  142 us
    all_gather x1, waiting for transfers between devices, shards(): lax.all_gather(part_feedforward, 'rep', axis=2, tiled=True)  97.3 us
  transfers between devices with their start and end apart: 9, of which 8 were waited for; matrix products, arithmetic and copies ran while one was open for 9% of the time, Pallas kernels for 0%

commit v1 on v0

--- a/solution.py
+++ b/solution.py
@@ -270,7 +270,10 @@
     )
     next_attention, next_feedforward, next_vectors = (
         lax.all_gather(part_attention, "rep", axis=2, tiled=True),
-        lax.all_gather(part_feedforward, "rep", axis=2, tiled=True),
+        jnp.concatenate(
+            lax.all_to_all(jnp.stack([part_feedforward] * lax.axis_size("rep")), "rep", 0, 0),
+            axis=2,
+        ),
         lax.all_gather(part_vectors, "rep", axis=1, tiled=True),
     )
     copy_attention = next_attention[2].astype(jnp.bfloat16)

time: 2360 us -> 2440 us (1.034)
  blocking collectives: 51.4 us -> 265 us
  waiting for transfers between devices: 2000 us -> 1850 us
    unnamed x1, blocking collectives: 12 us -> 226 us
    all_gather x1 -> x0, waiting for transfers between devices: 97.3 us -> none  [shards(): lax.all_gather(part_feedforward, 'rep', axis=2, tiled=True)]
    all_gather x1, waiting for transfers between devices: 35.4 us -> 0.01 us  [shards(): lax.all_gather(part_attention, 'rep', axis=2, tiled=True)]
  transfers between devices with their start and end apart: 9 -> 9, of which waited for: 8 -> 6; matrix products, arithmetic and copies ran while one was open for 9% -> 9% of each run, Pallas kernels for 0% -> 0%
where the time goes in v1:
time: 2440 us; the launch traced here: 2430 us
  waiting for transfers between devices  1850 us (76%)
  blocking collectives  265 us (11%)
  other arithmetic  117 us (5%)
  matrix products  89.5 us (4%)
  local copies, waits for them, and re-layouts  86.6 us (4%)
    reduce_scatter x1, waiting for transfers between devices, shards(): lax.psum_scatter(jnp.concatenate([contract_rows(layer_two, grad_pre), con...  811 us
    all_gather x1, waiting for transfers between devices, shards(): lax.all_gather(copies[1], 'fsdp', axis=0, tiled=True)  489 us
    reduce_scatter x1, waiting for transfers between devices, shards(): lax.psum_scatter(jnp.concatenate([contract_rows(layer_one, grad_qkv), con...  359 us
    unnamed x1, blocking collectives  226 us
    all_gather x1, waiting for transfers between devices, shards(): lax.all_gather(copies[0], 'fsdp', axis=0, tiled=True)  142 us
  transfers between devices with their start and end apart: 9, of which 6 were waited for; matrix products, arithmetic and copies ran while one was open for 9% of the time, Pallas kernels for 0%

profile of v1, /device:TPU:0, one launch (start us, length us, event | category | flops | bytes accessed | tf_op | source)
XLA Modules:
  0.0 2430.7 jit_solution(12266159200223745187)
XLA Ops:
  10.6 5.0 bitcast_convert_fusion
  17.1 33.6 %all-gather = bf16[8,160,12]{1,2,0:T(8,128)(2,1)S(1)} all-gather(bf16[1,160,12]{1,2,0:T(8,128)(2,1)S(1)} %copy.146), channel_id=1, replica_groups=mesh['rep'=4,'fsdp'=8] {'fsdp'}, dimensions={0}, use_global_device_ids=true | all-gather | bytes 34560 | tf_op jit(solution)/shard_map/all_gather | solution.py:93
  54.6 141.9 %all-gather.5.cloned.1.call-done = bf16[1280,5120]{1,0:T(8,128)(2,1)} async-done(((bf16[160,5120]{1,0:T(8,128)(2,1)}), bf16[1280,5120]{1,0:T(8,128)(2,1)}) %all-gather.5.cloned.1.call-update) | async-done | bytes 13107216 | tf_op jit(solution)/shard_map/all_gather | solution.py:91
  196.5 5.3 fusion.22
  203.5 3.7 fusion.121
  207.5 489.4 %all-gather.7.cloned.1.call-done = bf16[1280,10240]{1,0:T(8,128)(2,1)} async-done(((bf16[160,10240]{1,0:T(8,128)(2,1)}), bf16[1280,10240]{1,0:T(8,128)(2,1)}) %all-gather.7.cloned.1.call-update) | async-done | bytes 26214416 | tf_op jit(solution)/shard_map/all_gather | solution.py:92
  696.8 5.9 fusion.16
  702.8 11.3 convert_reduce_fusion
  714.1 8.1 multiply_reduce_fusion.1
  736.2 9.2 pad_maximum_fusion.1
  746.7 11.6 fusion.114
  758.3 12.3 fusion.109
  770.6 34.2 %pad_maximum_fusion = f32[1280,10240]{1,0:T(8,128)} fusion(f32[1280,5120]{1,0:T(8,128)} %fusion.109, f32[1280,5120]{1,0:T(8,128)} %fusion.114), kind=kLoop, calls=%fused_computation | loop fusion | flops 13107200 | bytes 104857600 | tf_op jit(solution)/shard_map/concatenate | solution.py:212
  804.9 359.0 %reduce-scatter.7.cloned.1.call-done = f32[160,5120]{1,0:T(8,128)} async-done(((f32[1280,5120]{1,0:T(8,128)}), f32[160,5120]{1,0:T(8,128)}) %reduce-scatter.7.cloned.1.call-update) | async-done | bytes 3276816 | tf_op jit(solution)/shard_map/reduce_scatter | solution.py:203
  1163.8 9.6 fusion.28
  1173.5 811.0 %reduce-scatter.9.cloned.1.call-done = f32[160,10240]{1,0:T(8,128)} async-done(((f32[1280,10240]{1,0:T(8,128)}), f32[160,10240]{1,0:T(8,128)}) %reduce-scatter.9.cloned.1.call-update) | async-done | bytes 6553616 | tf_op jit(solution)/shard_map/reduce_scatter | solution.py:211
  1984.5 18.2 fusion.15
  2003.2 6.5 fusion.116
  2009.8 6.0 fusion.86
  2021.0 12.6 fusion.115
  2033.6 22.5 reduce-scatter.15.cloned.1.call-done
  2061.5 12.0 stack.131
  2073.5 7.6 all-to-all-start
  2085.3 13.2 fusion.53
  2098.5 23.6 reduce-scatter.11.cloned.1.call-done
  2127.4 226.5 %all-reduce = bf16[12,160]{0,1:T(8,128)(2,1)S(1)} all-reduce(bf16[12,160]{0,1:T(8,128)(2,1)} %get-tuple-element.100), channel_id=7, replica_groups=mesh['rep'=4,'fsdp'=8] {'rep'}, use_global_device_ids=true, to_apply=%region_25.26.clone | all-reduce | flops 1920 | bytes 7680
  2354.2 5.4 all_gather.22
  2360.2 8.3 maximum_bitcast_fusion.2
  2371.8 17.0 maximum_bitcast_fusion
  2388.9 5.5 maximum_bitcast_fusion.1
  2394.4 17.1 copy.182
  2419.8 3.9 copy.187
  (169 shorter events, 57.3 us)
Async XLA Ops:
  7.2 44.4 %copy-start = (s32[1,8]{1,0:T(1,128)S(1)}, s32[1,8]{1,0:T(1,128)}, u32[]{:S(2)}) copy-start(s32[1,8]{1,0:T(1,128)} %param.12) | copy-start | bytes 100
  7.2 189.3 %all-gather.5.cloned.1.call-start = ((), (), s32[]{:S(2)}) async-start(), calls=%async_computation.6 | async-start | bytes 14745600 | tf_op jit(solution)/shard_map/all_gather | solution.py:91
  10.6 686.3 %all-gather.7.cloned.1.call-start = ((), (), s32[]{:S(2)}) async-start(), calls=%async_computation.7 | async-start | bytes 29491200 | tf_op jit(solution)/shard_map/all_gather | solution.py:92
  15.6 38.6 %copy-start.7 = (bf16[128,1280]{1,0:T(8,128)(2,1)S(1)}, bf16[128,1280]{1,0:T(8,128)(2,1)}, u32[]{:S(2)}) copy-start(bf16[128,1280]{1,0:T(8,128)(2,1)} %param.10) | copy-start | bytes 983044
  15.6 1148.2 %reduce-scatter.7.cloned.1.call-start = ((), (), s32[]{:S(2)}) async-start(), calls=%async_computation.8 | async-start | bytes 29491200 | tf_op jit(solution)/shard_map/reduce_scatter | solution.py:203
  17.1 184.8 %copy-start.12 = (f32[1,12,160]{1,2,0:T(8,128)}, f32[1,12,160]{1,2,0:T(8,128)S(1)}, u32[]{:S(2)}) copy-start(f32[1,12,160]{1,2,0:T(8,128)S(1)} %copy.177) | copy-start | bytes 23044
  207.2 538.3 %copy-start.6 = (f32[128,1280]{1,0:T(8,128)}, f32[128,1280]{1,0:T(8,128)S(1)}, u32[]{:S(2)}) copy-start(f32[128,1280]{1,0:T(8,128)S(1)} %get-tuple-element.138) | copy-start | bytes 1966084
  702.8 11.3 copy-start.26
  714.1 8.1 copy-start.10
  722.6 9.5 copy-start.4
  745.4 12.9 copy-start.20
  745.4 1239.1 %reduce-scatter.9.cloned.1.call-start = ((), (), s32[]{:S(2)}) async-start(), calls=%async_computation.9 | async-start | bytes 58982400 | tf_op jit(solution)/shard_map/reduce_scatter | solution.py:211
  746.7 11.6 copy-start.27
  804.8 1212.8 %reduce-scatter.13.cloned.1.call-start = ((), (), s32[]{:S(2)}) async-start(), calls=%async_computation.11 | async-start | bytes 2048000 | tf_op jit(solution)/shard_map/reduce_scatter | solution.py:231
  1173.5 882.7 %reduce-scatter.15.cloned.1.call-start = ((), (), s32[]{:S(2)}) async-start(), calls=%async_computation.13 | async-start | bytes 4096000 | tf_op jit(solution)/shard_map/reduce_scatter | solution.py:237
  2002.8 119.3 %reduce-scatter.11.cloned.1.call-start = ((), (), s32[]{:S(2)}) async-start(), calls=%async_computation.10 | async-start | bytes 737280 | tf_op jit(solution)/shard_map/reduce_scatter | solution.py:220
  2003.2 6.5 copy-start.9
  2003.2 6.5 copy-start.16
  2017.5 351.0 %all-gather.9.cloned.1.call-start = ((), (), s32[]{:S(2)}) async-start(), calls=%async_computation.12 | async-start | bytes 12288000 | tf_op jit(solution)/shard_map/all_gather | solution.py:272
  2073.5 7.7 copy-start.23
  2073.5 9.4 copy-start.25
  2073.5 10.6 copy-start.5
  2073.5 320.8 %all-to-all-start = ((f32[4,3,160,2560]{3,2,1,0:T(8,128)}), f32[4,3,160,2560]{3,2,1,0:T(8,128)}, u32[]{:S(2)}, u32[]{:S(2)}) async-start(f32[4,3,160,2560]{3,2,1,0:T(8,128)} %stack.131), calls=%async_computation.5 | async-start | bytes 39321600 | tf_op jit(solution)/shard_map/all_to_all | solution.py:274
  2085.3 36.8 %copy-start.13 = (f32[1,12,160]{1,2,0:T(8,128)S(1)}, f32[1,12,160]{1,2,0:T(8,128)}, u32[]{:S(2)}) copy-start(f32[1,12,160]{1,2,0:T(8,128)} %copy-done.12) | copy-start | bytes 23044
  2085.3 274.9 %copy-start.2 = (f32[160,5120]{1,0:T(8,128)S(1)}, f32[160,5120]{1,0:T(8,128)}, u32[]{:S(2)}) copy-start(f32[160,5120]{1,0:T(8,128)} %reduce-scatter.7.cloned.1.call-done) | copy-start | bytes 9830404
  2359.6 9.0 copy-start.21
  2371.8 17.0 slice-start
  2371.8 17.0 slice-start.1
  2371.8 17.0 copy-start.3
  2394.4 25.4 %slice-start.2 = ((s8[9830400]{0:T(1024)(128)(4,1)}), s8[4194304]{0:T(1024)(128)(4,1)S(1)}, s32[]{:S(2)}) async-start(s8[9830400]{0:T(1024)(128)(4,1)} %bitcast.217), calls=%async_computation.16 | async-start | bytes 8388608
  2394.4 25.4 %slice-start.3 = ((s8[9830400]{0:T(1024)(128)(4,1)}), s8[4194304]{0:T(1024)(128)(4,1)S(1)}, s32[]{:S(2)}) async-start(s8[9830400]{0:T(1024)(128)(4,1)} %bitcast.217), calls=%async_computation.17 | async-start | bytes 8388608
  2411.4 8.3 slice-start.4
  (10 other events, 27.4 us)
Sparse Core Ops, SparseCore 0:
  10.8 185.6 all-gather.4
  198.6 498.2 all-gather.6
  745.5 418.2 reduce-scatter.6
  1167.6 816.8 reduce-scatter.8
  1987.5 27.6 reduce-scatter.12
  2017.6 38.5 reduce-scatter.14
  2059.4 62.6 reduce-scatter.10
  2123.7 118.3 all-gather.8
